TPU v7x, 8 devices: a whole 2x2x1 slice. The times are simulated.
8 devices in a mesh: dp: 1 (over z), tp: 8 (over x, y, core).
Axes of the slice: x: 2, y: 2, z: 1, core: 2. Of those that a mesh axis runs over, the one named last changes fastest.
Arguments:
- x: bfloat16 [2048, 7168], P('dp')
- w_gate: bfloat16 [7168, 20480], P(None, 'tp')
- w_up: bfloat16 [7168, 20480], P(None, 'tp')
- w_down: bfloat16 [20480, 7168], P('tp')
Outputs:
- output: bfloat16 [2048, 7168], P('dp')
All inputs are finite; a program needn't handle non-finite values.
Results may differ from a plain program's by a relative error of at most 0.016.
Values are sent between devices in bfloat16 or wider.
A program may use at most 2 GiB of HBM per device.

v0:
```python
import jax
import jax.numpy as jnp
from jax import lax
from jax.sharding import PartitionSpec as P


def solution(mesh):
    def step(x, w_gate, w_up, w_down):
        gate = jnp.dot(x, w_gate, preferred_element_type=jnp.float32)
        up = jnp.dot(x, w_up, preferred_element_type=jnp.float32)
        hidden = (jax.nn.silu(gate) * up).astype(jnp.bfloat16)
        term = jnp.dot(hidden, w_down, preferred_element_type=jnp.float32).astype(jnp.bfloat16)
        return lax.psum(term, "tp")

    return jax.shard_map(
        step,
        mesh=mesh,
        in_specs=(P("dp", None), P(None, "tp"), P(None, "tp"), P("tp", None)),
        out_specs=P("dp", None),
        check_vma=False,
    )
```

profile of v0, /device:TPU:0, one launch (start us, length us, event | category | flops | bytes accessed | tf_op | source)
XLA Modules:
  0.0 639.2 jit_solution(4613552611251652953)
XLA Ops:
  6.5 0.0 all-reduce.2.cloned.1.call-start
  6.5 85.5 %fusion = f32[2048,2560]{1,0:T(8,128)} fusion(bf16[2048,7168]{1,0:T(8,128)(2,1)} %param.4, bf16[7168,2560]{1,0:T(8,128)(2,1)} %param.5), kind=kOutput, calls=%fused_computation.2 | convolution fusion | flops 75161927680 | bytes 87031808 | tf_op jit(solution)/shard_map/dot_general | solution.py:9
  92.1 91.4 %multiply_convert_fusion = bf16[2048,2560]{1,0:T(8,128)(2,1)} fusion(f32[2048,2560]{1,0:T(8,128)} %fusion, bf16[2048,7168]{1,0:T(8,128)(2,1)} %param.4, bf16[7168,2560]{1,0:T(8,128)(2,1)} %param.6), kind=kOutput, calls=%fused_computation.1 | convolution fusion | flops 75193384960 | bytes 97517568 | tf_op jit(solution)/shard_map/dot_general | solution.py:10
  183.5 85.1 %convolution_convert_fusion = bf16[2048,7168]{1,0:T(8,128)(2,1)} fusion(bf16[2048,2560]{1,0:T(8,128)(2,1)} %multiply_convert_fusion, bf16[2560,7168]{1,0:T(8,128)(2,1)} %param.7), kind=kOutput, calls=%fused_computation | convolution fusion | flops 75176607744 | bytes 76546048 | tf_op jit(solution)/shard_map/dot_general | solution.py:12
  268.6 0.0 all-reduce.2.cloned.1.call-update
  268.6 343.6 %all-reduce.2.cloned.1.call-done = bf16[2048,7168]{1,0:T(8,128)(2,1)} async-done(((bf16[2048,7168]{1,0:T(8,128)(2,1)}), bf16[2048,7168]{1,0:T(8,128)(2,1)}) %all-reduce.2.cloned.1.call-update) | async-done | bytes 29360144 | tf_op jit(solution)/shard_map/psum | solution.py:13
  612.2 20.1 %copy.6 = bf16[2048,7168]{1,0:T(8,128)(2,1)} copy(bf16[2048,7168]{1,0:T(8,128)(2,1)} %all-reduce.2.cloned.1.call-done) | data formatting | bytes 58720256
Async XLA Ops:
  6.5 605.6 %all-reduce.2.cloned.1.call-start = ((), (), s32[]{:S(2)}) async-start(), calls=%async_computation | async-start | bytes 58720256 | tf_op jit(solution)/shard_map/psum | solution.py:13
Sparse Core Ops, SparseCore 0:
  268.7 343.4 all-reduce.1
where the time goes:
time: 639 us
  waiting for transfers between devices  344 us (54%)
  matrix products  262 us (41%)
  local copies, waits for them, and re-layouts  20.1 us (3%)
  between operations  13.4 us (2%)
    psum x1, waiting for transfers between devices, step(): return lax.psum(term, 'tp')  344 us
    dot_general x1, matrix products, step(): up = jnp.dot(x, w_up, preferred_element_type=jnp.float32)  91.4 us
    dot_general x1, matrix products, step(): gate = jnp.dot(x, w_gate, preferred_element_type=jnp.float32)  85.5 us
    dot_general x1, matrix products, step(): jnp.dot(hidden, w_down, preferred_element_type=jnp.float32)  85.1 us
    unnamed x1, local copies, waits for them, and re-layouts  20.1 us
  transfers between devices with their start and end apart: 1, of which 1 were waited for; matrix products, arithmetic and copies ran while one was open for 0% of the time, Pallas kernels for 0%

commit v1 on v0

v1 whole, which is shorter than its diff:
```python
import jax
import jax.numpy as jnp
from jax import lax
from jax.sharding import PartitionSpec as P

CHUNKS = (256, 512, 640, 640)


def solution(mesh):
    def step(x, w_gate, w_up, w_down):
        outs = []
        start = 0
        for rows in CHUNKS:
            xs = x[start : start + rows]
            start += rows
            gate = jnp.dot(xs, w_gate, preferred_element_type=jnp.float32)
            up = jnp.dot(xs, w_up, preferred_element_type=jnp.float32)
            hidden = (jax.nn.silu(gate) * up).astype(jnp.bfloat16)
            term = jnp.dot(hidden, w_down, preferred_element_type=jnp.float32).astype(jnp.bfloat16)
            if outs:
                term, outs[-1] = lax.optimization_barrier((term, outs[-1]))
            outs.append(lax.psum(term, "tp"))
        return jnp.concatenate(outs, axis=0)

    return jax.shard_map(
        step,
        mesh=mesh,
        in_specs=(P("dp", None), P(None, "tp"), P(None, "tp"), P("tp", None)),
        out_specs=P("dp", None),
        check_vma=False,
    )
```

time: 639 us -> 596 us (0.933); the launches traced: 639 us -> 588 us
  waiting for transfers between devices: 344 us -> 239 us
  matrix products: 262 us -> 315 us
  local copies, waits for them, and re-layouts: 20.1 us -> 0 us
  other arithmetic: 0 us -> 20 us
    psum x1 -> x4, waiting for transfers between devices: 344 us -> 239 us  [step(): outs.append(lax.psum(term, 'tp'))]
    dot_general x2 -> x8, matrix products: 177 us -> 211 us  [the longest x4 107 us: step(): up = jnp.dot(xs, w_up, preferred_element_type=jnp.float32)]
    unnamed x1 -> x0, local copies, waits for them, and re-layouts: 20.1 us -> none
    concatenate x0 -> x1, other arithmetic: none -> 20 us  [step(): return jnp.concatenate(outs, axis=0)]
    dot_general x1 -> x4, matrix products: 85.1 us -> 104 us  [step(): jnp.dot(hidden, w_down, preferred_element_type=jnp.float32)]
  transfers between devices with their start and end apart: 1 -> 4, of which waited for: 1 -> 3; matrix products, arithmetic and copies ran while one was open for 0% -> 44% of each run, Pallas kernels for 0% -> 0%
where the time goes in v1:
time: 596 us; the launch traced here: 588 us
  matrix products  315 us (53%)
  waiting for transfers between devices  239 us (40%)
  other arithmetic  20 us (3%)
  between operations  13.6 us (2%)
    psum x4, waiting for transfers between devices, step(): outs.append(lax.psum(term, 'tp'))  239 us
    dot_general x4, matrix products, step(): up = jnp.dot(xs, w_up, preferred_element_type=jnp.float32)  107 us
    dot_general x4, matrix products, step(): gate = jnp.dot(xs, w_gate, preferred_element_type=jnp.float32)  105 us
    dot_general x4, matrix products, step(): jnp.dot(hidden, w_down, preferred_element_type=jnp.float32)  104 us
    concatenate x1, other arithmetic, step(): return jnp.concatenate(outs, axis=0)  20 us
  transfers between devices with their start and end apart: 4, of which 3 were waited for; matrix products, arithmetic and copies ran while one was open for 44% of the time, Pallas kernels for 0%

profile of v1, /device:TPU:0, one launch (start us, length us, event | category | flops | bytes accessed | tf_op | source)
XLA Modules:
  0.0 588.0 jit_solution(4580079702935534783)
XLA Ops:
  6.5 0.0 all-reduce.5.cloned.1.call-start
  6.5 17.4 %fusion.21 = f32[256,2560]{1,0:T(8,128)S(1)} fusion(bf16[7168,2560]{1,0:T(8,128)(2,1)} %param.5, bf16[2048,7168]{1,0:T(8,128)(2,1)} %param.4), kind=kOutput, calls=%fused_computation.23 | convolution fusion | flops 9395240960 | bytes 42991616 | tf_op jit(solution)/shard_map/dot_general | solution.py:16
  23.9 18.3 %fusion.18.clone.4 = bf16[256,2560]{1,0:T(8,128)(2,1)} fusion(bf16[7168,2560]{1,0:T(8,128)(2,1)} %param.6, bf16[2048,7168]{1,0:T(8,128)(2,1)} %param.4, f32[256,2560]{1,0:T(8,128)S(1)} %fusion.21), kind=kOutput, calls=%fused_computation.21.clone.clone.clone.1 | convolution fusion | flops 9399173120 | bytes 44302336 | tf_op jit(solution)/shard_map/dot_general | solution.py:17
  42.2 18.0 %convolution_convert_fusion.3 = bf16[256,7168]{1,0:T(8,128)(2,1)} fusion(bf16[2560,7168]{1,0:T(8,128)(2,1)} %param.7, bf16[256,2560]{1,0:T(8,128)(2,1)} %fusion.18.clone.4), kind=kOutput, calls=%fused_computation.4 | convolution fusion | flops 9397075968 | bytes 41680896 | tf_op jit(solution)/shard_map/dot_general | solution.py:19
  60.2 0.0 all-reduce.5.cloned.1.call-update
  60.2 0.2 all-reduce.7.cloned.1.call-start
  60.5 24.0 %fusion.10 = f32[512,2560]{1,0:T(8,128)S(1)} fusion(bf16[7168,2560]{1,0:T(8,128)(2,1)} %param.5, bf16[2048,7168]{1,0:T(8,128)(2,1)} %param.4), kind=kOutput, calls=%fused_computation.17 | convolution fusion | flops 18790481920 | bytes 49283072 | tf_op jit(solution)/shard_map/dot_general | solution.py:16
  84.4 31.7 %fusion.2 = f32[640,2560]{1,0:T(8,128)} fusion(bf16[7168,2560]{1,0:T(8,128)(2,1)} %param.5, bf16[2048,7168]{1,0:T(8,128)(2,1)} %param.4), kind=kOutput, calls=%fused_computation.7 | convolution fusion | flops 23488102400 | bytes 52428800 | tf_op jit(solution)/shard_map/dot_general | solution.py:16
  116.2 31.4 %fusion.6 = f32[640,2560]{1,0:T(8,128)} fusion(bf16[7168,2560]{1,0:T(8,128)(2,1)} %param.5, bf16[2048,7168]{1,0:T(8,128)(2,1)} %param.4), kind=kOutput, calls=%fused_computation.11 | convolution fusion | flops 23488102400 | bytes 52428800 | tf_op jit(solution)/shard_map/dot_general | solution.py:16
  147.6 25.5 %multiply_convert_fusion.2 = bf16[512,2560]{1,0:T(8,128)(2,1)S(1)} fusion(f32[512,2560]{1,0:T(8,128)S(1)} %fusion.10, bf16[7168,2560]{1,0:T(8,128)(2,1)} %param.6, bf16[2048,7168]{1,0:T(8,128)(2,1)} %param.4), kind=kOutput, calls=%fused_computation.19 | convolution fusion | flops 18798346240 | bytes 51904512 | tf_op jit(solution)/shard_map/dot_general | solution.py:17
  173.2 27.2 %convolution_convert_fusion.2 = bf16[512,7168]{1,0:T(8,128)(2,1)} fusion(bf16[512,2560]{1,0:T(8,128)(2,1)S(1)} %multiply_convert_fusion.2, bf16[2560,7168]{1,0:T(8,128)(2,1)} %param.7), kind=kOutput, calls=%fused_computation.3 | convolution fusion | flops 18794151936 | bytes 46661632 | tf_op jit(solution)/shard_map/dot_general | solution.py:19
  200.4 0.0 all-reduce.5.cloned.1.call-done
  200.4 0.0 all-reduce.7.cloned.1.call-update
  200.4 0.0 all-reduce.9.cloned.1.call-start
  200.5 31.3 %multiply_convert_fusion.1 = bf16[640,2560]{1,0:T(8,128)(2,1)S(1)} fusion(f32[640,2560]{1,0:T(8,128)} %fusion.6, bf16[7168,2560]{1,0:T(8,128)(2,1)} %param.6, bf16[2048,7168]{1,0:T(8,128)(2,1)} %param.4), kind=kOutput, calls=%fused_computation.14 | convolution fusion | flops 23497932800 | bytes 55705600 | tf_op jit(solution)/shard_map/dot_general | solution.py:17
  231.8 29.4 %convolution_convert_fusion.1 = bf16[640,7168]{1,0:T(8,128)(2,1)} fusion(bf16[640,2560]{1,0:T(8,128)(2,1)S(1)} %multiply_convert_fusion.1, bf16[2560,7168]{1,0:T(8,128)(2,1)} %param.7), kind=kOutput, calls=%fused_computation.2 | convolution fusion | flops 23492689920 | bytes 49152000 | tf_op jit(solution)/shard_map/dot_general | solution.py:19
  261.2 46.2 %all-reduce.7.cloned.1.call-done = bf16[512,7168]{1,0:T(8,128)(2,1)} async-done(((bf16[512,7168]{1,0:T(8,128)(2,1)}), bf16[512,7168]{1,0:T(8,128)(2,1)}) %all-reduce.7.cloned.1.call-update) | async-done | bytes 7340048 | tf_op jit(solution)/shard_map/psum | solution.py:22
  307.3 0.0 all-reduce.9.cloned.1.call-update
  307.4 0.0 all-reduce.11.cloned.1.call-start
  307.4 31.6 %multiply_convert_fusion = bf16[640,2560]{1,0:T(8,128)(2,1)S(1)} fusion(f32[640,2560]{1,0:T(8,128)} %fusion.2, bf16[7168,2560]{1,0:T(8,128)(2,1)} %param.6, bf16[2048,7168]{1,0:T(8,128)(2,1)} %param.4), kind=kOutput, calls=%fused_computation.13 | convolution fusion | flops 23497932800 | bytes 55705600 | tf_op jit(solution)/shard_map/dot_general | solution.py:17
  339.0 29.3 %convolution_convert_fusion = bf16[640,7168]{1,0:T(8,128)(2,1)} fusion(bf16[640,2560]{1,0:T(8,128)(2,1)S(1)} %multiply_convert_fusion, bf16[2560,7168]{1,0:T(8,128)(2,1)} %param.7), kind=kOutput, calls=%fused_computation.1 | convolution fusion | flops 23492689920 | bytes 49152000 | tf_op jit(solution)/shard_map/dot_general | solution.py:19
  368.4 65.9 %all-reduce.9.cloned.1.call-done = bf16[640,7168]{1,0:T(8,128)(2,1)} async-done(((bf16[640,7168]{1,0:T(8,128)(2,1)}), bf16[640,7168]{1,0:T(8,128)(2,1)}) %all-reduce.9.cloned.1.call-update) | async-done | bytes 9175056 | tf_op jit(solution)/shard_map/psum | solution.py:22
  434.3 0.0 all-reduce.11.cloned.1.call-update
  434.3 126.7 %all-reduce.11.cloned.1.call-done = bf16[640,7168]{1,0:T(8,128)(2,1)} async-done(((bf16[640,7168]{1,0:T(8,128)(2,1)}), bf16[640,7168]{1,0:T(8,128)(2,1)}) %all-reduce.11.cloned.1.call-update) | async-done | bytes 9175056 | tf_op jit(solution)/shard_map/psum | solution.py:22
  561.0 20.0 %pad_maximum_fusion = bf16[2048,7168]{1,0:T(8,128)(2,1)} fusion(bf16[640,7168]{1,0:T(8,128)(2,1)} %all-reduce.11.cloned.1.call-done, bf16[640,7168]{1,0:T(8,128)(2,1)} %all-reduce.9.cloned.1.call-done, bf16[512,7168]{1,0:T(8,128)(2,1)} %all-reduce.7.cloned.1.call-done, bf16[256,7168]{1,0:T(8,128)(2,1)} %all-reduce.5.cloned.1.call-done), kind=kLoop, calls=%fused_computation | loop fusion | flops 117440512 | bytes 58720256 | tf_op jit(solution)/shard_map/concatenate | solution.py:23
Async XLA Ops:
  6.5 193.9 %all-reduce.5.cloned.1.call-start = ((), (), s32[]{:S(2)}) async-start(), calls=%async_computation | async-start | bytes 7340032 | tf_op jit(solution)/shard_map/psum | solution.py:22
  60.2 247.1 %all-reduce.7.cloned.1.call-start = ((), (), s32[]{:S(2)}) async-start(), calls=%async_computation.1 | async-start | bytes 14680064 | tf_op jit(solution)/shard_map/psum | solution.py:22
  200.4 233.9 %all-reduce.9.cloned.1.call-start = ((), (), s32[]{:S(2)}) async-start(), calls=%async_computation.2 | async-start | bytes 18350080 | tf_op jit(solution)/shard_map/psum | solution.py:22
  307.4 253.7 %all-reduce.11.cloned.1.call-start = ((), (), s32[]{:S(2)}) async-start(), calls=%async_computation.3 | async-start | bytes 18350080 | tf_op jit(solution)/shard_map/psum | solution.py:22
Sparse Core Ops, SparseCore 0:
  60.4 66.3 all-reduce.4
  200.5 106.7 all-reduce.6
  310.9 123.3 all-reduce.8
  437.7 123.2 all-reduce.10

commit v2 on v0

v2 whole, which is shorter than its diff:
```python
import functools

import jax
import jax.numpy as jnp
from jax import lax
from jax.experimental import pallas as pl
from jax.experimental.pallas import tpu as pltpu
from jax.sharding import PartitionSpec as P

BF16 = jnp.bfloat16
F32 = jnp.float32
R = 512
GT = 256
W = 512
MESH = pl.DeviceIdType.MESH


def kernel(
    n_chunks, n_gu, n_u,
    x_hbm, wg_hbm, wu_hbm, wd_hbm, y_hbm,
    xbuf, hid, wgu, wdb, obuf, orecv, sbuf, r1, r2,
    x_sem, wgu_sem, wd_sem, o_ss, o_rs, r1_ss, r1_rs, r2_ss, r2_rs,
    a1_ss, a1_rs, a2_ss, a2_rs, a3_ss, a3_rs, loc_sem, d_ss, d_rs, credit,
):
    me = lax.axis_index("tp")
    dp = lax.axis_index("dp")
    c = lax.rem(me, 2)
    cy = lax.rem(me // 2, 2)
    cx = me // 4
    partner = me + 1 - 2 * c
    xn = me + 4 - 8 * cx
    yn = me + 2 - 4 * cy
    half = n_u * W
    n_dn = 2 * n_u
    q, h = R // 8, R // 4

    def dev(i):
        return (dp, i)

    def x_copy(i):
        return pltpu.make_async_copy(x_hbm.at[pl.ds(i * R, R), :], xbuf, x_sem)

    def gu_copies(g):
        slot = lax.rem(g, 2)
        col = pl.multiple_of(lax.rem(g, n_gu) * GT, GT)
        return [
            pltpu.make_async_copy(
                w.at[:, pl.ds(col, GT)], wgu.at[slot, :, pl.ds(k * GT, GT)], wgu_sem.at[slot, k]
            )
            for k, w in enumerate((wg_hbm, wu_hbm))
        ]

    def wd_copy(g):
        n = lax.rem(g, n_dn)
        slot = lax.rem(g, 3)
        odd = lax.rem(n, 2) == 1
        last = n == n_dn - 1
        own = jnp.logical_or(last, jnp.logical_and(jnp.logical_not(odd), n > 0))
        tile = jnp.where(last, n_u - 1, jnp.where(odd, (n + 1) // 2, jnp.maximum(n // 2 - 1, 0)))
        col = pl.multiple_of(jnp.where(own, c, 1 - c) * half + tile * W, W)
        return pltpu.make_async_copy(wd_hbm.at[:, pl.ds(col, W)], wdb.at[slot], wd_sem.at[slot])

    def remote(src, dst, ss, rs, to):
        return pltpu.make_async_remote_copy(
            src_ref=src, dst_ref=dst, send_sem=ss, recv_sem=rs, device_id=dev(to), device_id_type=MESH
        )

    def o_send(u):
        return remote(obuf.at[u], orecv.at[u], o_ss.at[u], o_rs.at[u], partner)

    first = (xn, yn)
    second = (yn, xn)
    f_bit = (cx, cy)
    s_bit = (cy, cx)

    def keep1(k):
        return pl.multiple_of(k * (R // 2) + f_bit[k] * h, h)

    def give1(k):
        return pl.multiple_of(k * (R // 2) + (1 - f_bit[k]) * h, h)

    def keep2(k):
        return pl.multiple_of(keep1(k) + s_bit[k] * q, q)

    def give2(k):
        return pl.multiple_of(keep1(k) + (1 - s_bit[k]) * q, q)

    def rs1(k, u):
        return remote(
            sbuf.at[u, pl.ds(give1(k), h), :], r1.at[k, u], r1_ss.at[k, u], r1_rs.at[k, u], first[k]
        )

    def rs2(k, u):
        return remote(
            sbuf.at[u, pl.ds(give2(k), q), :], r2.at[k, u], r2_ss.at[k, u], r2_rs.at[k, u], second[k]
        )

    def place(i, u, row, rows):
        col = pl.multiple_of(c * half + u * W, W)
        return y_hbm.at[pl.ds(pl.multiple_of(i * R + row, q), rows), pl.ds(col, W)]

    def ag1(k, i, u):
        return remote(
            sbuf.at[u, pl.ds(keep2(k), q), :], place(i, u, keep2(k), q),
            a1_ss.at[k, u], a1_rs.at[k, u], second[k],
        )

    def ag2(k, i, u):
        return remote(
            sbuf.at[u, pl.ds(keep2(k), q), :], place(i, u, keep2(k), q),
            a2_ss.at[k, u], a2_rs.at[k, u], first[k],
        )

    def ag3(k, i, u):
        at = place(i, u, give2(k), q)
        return remote(at, at, a3_ss.at[k, u], a3_rs.at[k, u], first[k])

    def local(k, i, u):
        return pltpu.make_async_copy(
            sbuf.at[u, pl.ds(keep2(k), q), :], place(i, u, keep2(k), q), loc_sem.at[k, u]
        )

    def across(i, u):
        at = place(i, u, 0, R)
        return remote(at, at, d_ss.at[i, u], d_rs.at[i, u], partner)

    def p1(i, u):
        for k in range(2):
            rs1(k, u).wait_recv()
            rows = pl.ds(keep1(k), h)
            sbuf[u, rows, :] = (sbuf[u, rows, :].astype(F32) + r1[k, u].astype(F32)).astype(BF16)
            rs2(k, u).start()

    def p2(i, u):
        for k in range(2):
            rs2(k, u).wait_recv()
            rows = pl.ds(keep2(k), q)
            sbuf[u, rows, :] = (sbuf[u, rows, :].astype(F32) + r2[k, u].astype(F32)).astype(BF16)
            ag1(k, i, u).start()
            ag2(k, i, u).start()
            local(k, i, u).start()

    def p3(i, u):
        for k in range(2):
            ag1(k, i, u).wait_recv()
            ag3(k, i, u).start()

    def p4(i, u):
        for k in range(2):
            ag2(k, i, u).wait_recv()
            ag3(k, i, u).wait_recv()
            local(k, i, u).wait()
            rs1(k, u).wait_send()
            rs2(k, u).wait_send()
            ag1(k, i, u).wait_send()
            ag2(k, i, u).wait_send()
            ag3(k, i, u).wait_send()
        across(i, u).start()

    def loop(lo, hi, f):
        def body(s, carry):
            f(s)
            return carry

        lax.fori_loop(lo, hi, body, 0)

    x_copy(0).start()
    for g in range(2):
        for cp in gu_copies(g):
            cp.start()
    for g in range(3):
        wd_copy(g).start()
    barrier = pltpu.get_barrier_semaphore()
    for other in (partner, xn, yn):
        pl.semaphore_signal(barrier, inc=1, device_id=dev(other), device_id_type=MESH)
    pl.semaphore_wait(barrier, 3)

    def chunk(i):
        x_copy(i).wait()
        prev = i - 1

        def gu(j):
            g = i * n_gu + j

            @pl.when(i > 0)
            def _():
                @pl.when(j == 0)
                def _():
                    loop(n_u - 2, n_u, lambda u: p1(prev, u))

                loop(jnp.minimum(2 * j, n_u), jnp.minimum(2 * j + 2, n_u), lambda u: p2(prev, u))
                b = 2 * jnp.maximum(j - 3, 0)
                t = 2 * jnp.maximum(j - 2, 0)
                loop(jnp.minimum(b, n_u), jnp.minimum(t, n_u), lambda u: p3(prev, u))

            slot = lax.rem(g, 2)
            for cp in gu_copies(g):
                cp.wait()
            r = jnp.dot(xbuf[...], wgu[slot], preferred_element_type=F32)
            gate, up = r[:, :GT], r[:, GT:]
            hid[:, pl.ds(pl.multiple_of(j * GT, GT), GT)] = (jax.nn.silu(gate) * up).astype(BF16)

            @pl.when(g + 2 < n_chunks * n_gu)
            def _():
                for cp in gu_copies(g + 2):
                    cp.start()

        loop(0, n_gu, gu)

        @pl.when(i + 1 < n_chunks)
        def _():
            x_copy(i + 1).start()

        def next_wd(g):
            @pl.when(g + 3 < n_chunks * n_dn)
            def _():
                wd_copy(g + 3).start()

        def down(k):
            @pl.when(k < n_u)
            def _():
                @pl.when(i > 0)
                def _():
                    o_send(k).wait_send()

                    @pl.when(k == 0)
                    def _():
                        pl.semaphore_wait(credit, 1)

                g = i * n_dn + jnp.maximum(2 * k - 1, 0)
                wd_copy(g).wait()
                r = jnp.dot(hid[...], wdb[lax.rem(g, 3)], preferred_element_type=F32)
                obuf[k] = r.astype(BF16)
                o_send(k).start()
                next_wd(g)

            @pl.when(k > 0)
            def _():
                u = k - 1

                @pl.when(i > 0)
                def _():
                    p4(prev, u)

                g = i * n_dn + jnp.minimum(2 * k, n_dn - 1)
                wd_copy(g).wait()
                o_send(u).wait_recv()
                r = jnp.dot(hid[...], wdb[lax.rem(g, 3)], preferred_element_type=F32)
                sbuf[u] = (r + orecv[u].astype(F32)).astype(BF16)
                for color in range(2):
                    rs1(color, u).start()
                next_wd(g)

            @pl.when(k > 2)
            def _():
                p1(i, k - 3)

        loop(0, n_u + 1, down)

        @pl.when(i + 1 < n_chunks)
        def _():
            pl.semaphore_signal(credit, inc=1, device_id=dev(partner), device_id_type=MESH)

    loop(0, n_chunks, chunk)

    end = n_chunks - 1
    loop(n_u - 2, n_u, lambda u: p1(end, u))

    def tail(s):
        @pl.when(s < n_u)
        def _():
            p2(end, s)

        @pl.when(jnp.logical_and(s >= 2, s < n_u + 2))
        def _():
            p3(end, s - 2)

        @pl.when(s >= 4)
        def _():
            p4(end, s - 4)

    loop(0, n_u + 4, tail)

    def drain(u):
        o_send(u).wait_send()

        def one(i):
            across(i, u).wait_send()
            across(i, u).wait_recv()

        loop(0, n_chunks, one)

    loop(0, n_u, drain)


def solution(mesh):
    def step(x, w_gate, w_up, w_down):
        rows, d = x.shape
        ff = w_gate.shape[1]
        n_chunks, n_gu, n_u = rows // R, ff // GT, d // (2 * W)
        dma = pltpu.SemaphoreType.DMA
        pair = (2, n_u)
        any_space = pl.BlockSpec(memory_space=pl.ANY)
        return pl.pallas_call(
            functools.partial(kernel, n_chunks, n_gu, n_u),
            out_shape=jax.ShapeDtypeStruct((rows, d), BF16),
            in_specs=[any_space] * 4,
            out_specs=any_space,
            scratch_shapes=[
                pltpu.VMEM((R, d), BF16),
                pltpu.VMEM((R, ff), BF16),
                pltpu.VMEM((2, d, 2 * GT), BF16),
                pltpu.VMEM((3, ff, W), BF16),
                pltpu.VMEM((n_u, R, W), BF16),
                pltpu.VMEM((n_u, R, W), BF16),
                pltpu.VMEM((n_u, R, W), BF16),
                pltpu.VMEM((2, n_u, R // 4, W), BF16),
                pltpu.VMEM((2, n_u, R // 8, W), BF16),
                dma, dma((2, 2)), dma((3,)),
                dma((n_u,)), dma((n_u,)),
                *[dma(pair) for _ in range(10)],
                dma(pair),
                dma((n_chunks, n_u)), dma((n_chunks, n_u)),
                pltpu.SemaphoreType.REGULAR,
            ],
            compiler_params=pltpu.CompilerParams(
                collective_id=0, has_side_effects=True, vmem_limit_bytes=62 * 1024 * 1024
            ),
            name="mlp_reduce",
        )(x, w_gate, w_up, w_down)

    return jax.shard_map(
        step,
        mesh=mesh,
        in_specs=(P("dp", None), P(None, "tp"), P(None, "tp"), P("tp", None)),
        out_specs=P("dp", None),
        check_vma=False,
    )
```

time: 639 us -> 366 us (0.57)
  Pallas kernels: 0 us -> 345 us
  waiting for transfers between devices: 344 us -> 0 us
  matrix products: 262 us -> 0 us
  between operations: 13.4 us -> 0.01 us
    pallas_call x0 -> x1, Pallas kernels: none -> 345 us  [step(): pl.pallas_call(functools.partial(kernel, n_chunks, n_gu, n_u), out_shape=...]
    psum x1 -> x0, waiting for transfers between devices: 344 us -> none  [step(): return lax.psum(term, 'tp')]
    dot_general x3 -> x0, matrix products: 262 us -> none  [the longest x1 91.4 us: step(): up = jnp.dot(x, w_up, preferred_element_type=jnp.float32)]
  transfers between devices with their start and end apart: 1 -> 0, of which waited for: 1 -> 0; matrix products, arithmetic and copies ran while one was open for 0% -> 0% of each run, Pallas kernels for 0% -> 0%
where the time goes in v2:
time: 366 us
  Pallas kernels  345 us (94%)
  local copies, waits for them, and re-layouts  20.2 us (6%)
    pallas_call x1, Pallas kernels, step(): pl.pallas_call(functools.partial(kernel, n_chunks, n_gu, n_u), out_shape=...  345 us
    unnamed x1, local copies, waits for them, and re-layouts  20.2 us

profile of v2, /device:TPU:0, one launch (start us, length us, event | category | flops | bytes accessed | tf_op | source)
XLA Modules:
  0.0 365.6 jit_solution(735642311126086335)
XLA Ops:
  0.0 345.5 %mlp_reduce.1 = bf16[2048,7168]{1,0:T(8,128)(2,1)} custom-call(bf16[2048,7168]{1,0:T(8,128)(2,1)} %x_hbm.1, bf16[7168,2560]{1,0:T(8,128)(2,1)} %wg_hbm.1, bf16[7168,2560]{1,0:T(8,128)(2,1)} %wu_hbm.1, bf16[2560,7168]{1,0:T(8,128)(2,1)} %wd_hbm.1), custom_call_target="tpu_custom_call" | custom-call | tf_op jit(solution)/shard_map/mlp_reduce/pallas_call | solution.py:304
  345.5 20.2 %copy.6 = bf16[2048,7168]{1,0:T(8,128)(2,1)} copy(bf16[2048,7168]{1,0:T(8,128)(2,1)} %mlp_reduce.1) | data formatting | bytes 58720256

commit v3 on v0

v3 whole, which is shorter than its diff:
```python
import functools

import jax
import jax.numpy as jnp
from jax import lax
from jax.experimental import pallas as pl
from jax.experimental.pallas import tpu as pltpu
from jax.sharding import PartitionSpec as P

BF16 = jnp.bfloat16
F32 = jnp.float32
MAIN, LAST = 448, 256
GT = 256
W = 512
V = W // 2
SLOTS = 4
END_P1, END_P2 = 5, 8
D2, D3, D4 = 1, 3, 5
O_LEAD = 2
P1_LAG = 8
P2_AT, P3_AT, P3_EACH = 3, 8, 4
MESH = pl.DeviceIdType.MESH


def when(cond, f):
    if isinstance(cond, bool):
        if cond:
            f()
    else:
        pl.when(cond)(f)


def loop(lo, hi, f):
    def body(s, carry):
        f(s)
        return carry

    lax.fori_loop(lo, hi, body, 0)


def kernel(
    n_main, n_gu, n_u,
    x_hbm, wg_hbm, wu_hbm, wd_hbm, y_hbm,
    xbuf, hid, wgu, wdb, obuf, orecv, sbuf, r1, r2,
    x_sem, wgu_sem, wd_sem, o_ss, o_rs, r1_ss, r1_rs, r2_ss, r2_rs,
    a1_ss, a1_rs, a2_ss, a2_rs, a3_ss, a3_rs, loc_sem, d_ss, d_rs, credit,
):
    me = lax.axis_index("tp")
    dp = lax.axis_index("dp")
    c = lax.rem(me, 2)
    cy = lax.rem(me // 2, 2)
    cx = me // 4
    partner = me + 1 - 2 * c
    xn = me + 4 - 8 * cx
    yn = me + 2 - 4 * cy
    half = n_u * W
    n_dn = 2 * n_u
    n_chunks = n_main + 1

    def dev(i):
        return (dp, i)

    def size(i):
        return LAST if isinstance(i, int) and i == n_main else MAIN

    def x_copy(i):
        rows = size(i)
        at = pl.ds(pl.multiple_of(i * MAIN, MAIN), rows)
        slot = lax.rem(jnp.int32(i), 2)
        return pltpu.make_async_copy(x_hbm.at[at, :], xbuf.at[slot, pl.ds(0, rows), :], x_sem.at[slot])

    def gu_copies(g):
        slot = lax.rem(g, 2)
        col = pl.multiple_of(lax.rem(g, n_gu) * GT, GT)
        return [
            pltpu.make_async_copy(
                w.at[:, pl.ds(col, GT)], wgu.at[slot, :, pl.ds(k * GT, GT)], wgu_sem.at[slot, k]
            )
            for k, w in enumerate((wg_hbm, wu_hbm))
        ]

    def o_index(u):
        return jnp.maximum(2 * u - O_LEAD, jnp.minimum(u, O_LEAD))

    def w_index(u):
        return jnp.minimum(2 * u + O_LEAD + 1, n_u + u)

    def wd_copy(g):
        n = lax.rem(g, n_dn)
        slot = lax.rem(g, SLOTS)
        m = n - O_LEAD
        head, tail = n < O_LEAD, n >= n_dn - O_LEAD
        even = lax.rem(m + 2 * O_LEAD, 2) == 0
        own = jnp.logical_or(tail, jnp.logical_and(jnp.logical_not(head), jnp.logical_not(even)))
        mid = jnp.where(even, O_LEAD + m // 2, m // 2)
        tile = jnp.where(head, n, jnp.where(tail, n - n_u, mid))
        col = pl.multiple_of(jnp.where(own, c, 1 - c) * half + tile * W, W)
        return pltpu.make_async_copy(wd_hbm.at[:, pl.ds(col, W)], wdb.at[slot], wd_sem.at[slot])

    def remote(src, dst, ss, rs, to):
        return pltpu.make_async_remote_copy(
            src_ref=src, dst_ref=dst, send_sem=ss, recv_sem=rs, device_id=dev(to), device_id_type=MESH
        )

    def o_send(i, u):
        rows = pl.ds(0, size(i))
        return remote(obuf.at[u, rows, :], orecv.at[u, rows, :], o_ss.at[u], o_rs.at[u], partner)

    first = (xn, yn)
    second = (yn, xn)
    f_bit = (cx, cy)
    s_bit = (cy, cx)

    def keep1(i, k):
        h = size(i) // 2
        return pl.multiple_of(f_bit[k] * h, h)

    def give1(i, k):
        h = size(i) // 2
        return pl.multiple_of((1 - f_bit[k]) * h, h)

    def keep2(i, k):
        q = size(i) // 4
        return pl.multiple_of(keep1(i, k) + s_bit[k] * q, q)

    def give2(i, k):
        q = size(i) // 4
        return pl.multiple_of(keep1(i, k) + (1 - s_bit[k]) * q, q)

    def rs1(i, k, u):
        h = size(i) // 2
        return remote(
            sbuf.at[k, u, pl.ds(give1(i, k), h), :], r1.at[k, u, pl.ds(0, h), :],
            r1_ss.at[k, u], r1_rs.at[k, u], first[k],
        )

    def rs2(i, k, u):
        q = size(i) // 4
        return remote(
            sbuf.at[k, u, pl.ds(give2(i, k), q), :], r2.at[k, u, pl.ds(0, q), :],
            r2_ss.at[k, u], r2_rs.at[k, u], second[k],
        )

    def place(i, k, u, row):
        q = size(i) // 4
        col = pl.multiple_of(c * half + u * W + k * V, V)
        return y_hbm.at[pl.ds(pl.multiple_of(i * MAIN + row, q), q), pl.ds(col, V)]

    def piece(i, k, u):
        q = size(i) // 4
        return sbuf.at[k, u, pl.ds(keep2(i, k), q), :], place(i, k, u, keep2(i, k))

    def ag1(i, k, u):
        return remote(*piece(i, k, u), a1_ss.at[k, u], a1_rs.at[k, u], second[k])

    def ag2(i, k, u):
        return remote(*piece(i, k, u), a2_ss.at[k, u], a2_rs.at[k, u], first[k])

    def ag3(i, k, u):
        at = place(i, k, u, give2(i, k))
        return remote(at, at, a3_ss.at[k, u], a3_rs.at[k, u], first[k])

    def local(i, k, u):
        return pltpu.make_async_copy(*piece(i, k, u), loc_sem.at[k, u])

    def across(i, u):
        col = pl.multiple_of(c * half + u * W, W)
        at = y_hbm.at[pl.ds(pl.multiple_of(i * MAIN, MAIN), size(i)), pl.ds(col, W)]
        return remote(at, at, d_ss.at[i, u], d_rs.at[i, u], partner)

    def p1(i, u):
        h = size(i) // 2
        for k in range(2):
            rs1(i, k, u).wait_recv()
            rows = pl.ds(keep1(i, k), h)
            sbuf[k, u, rows, :] = (sbuf[k, u, rows, :].astype(F32) + r1[k, u, :h].astype(F32)).astype(BF16)
            rs2(i, k, u).start()

    def p2(i, u):
        q = size(i) // 4
        for k in range(2):
            rs2(i, k, u).wait_recv()
            rows = pl.ds(keep2(i, k), q)
            sbuf[k, u, rows, :] = (sbuf[k, u, rows, :].astype(F32) + r2[k, u, :q].astype(F32)).astype(BF16)
            ag1(i, k, u).start()
            ag2(i, k, u).start()
            local(i, k, u).start()

    def p3(i, u):
        for k in range(2):
            ag1(i, k, u).wait_recv()
            ag3(i, k, u).start()

    def p4(i, u):
        for k in range(2):
            ag2(i, k, u).wait_recv()
            ag3(i, k, u).wait_recv()
            local(i, k, u).wait()
            rs1(i, k, u).wait_send()
            rs2(i, k, u).wait_send()
            ag1(i, k, u).wait_send()
            ag2(i, k, u).wait_send()
            ag3(i, k, u).wait_send()
        across(i, u).start()

    p1_left = n_u + O_LEAD - P1_LAG

    x_copy(0).start()
    for g in range(2):
        for cp in gu_copies(g):
            cp.start()
    for g in range(SLOTS):
        wd_copy(g).start()
    barrier = pltpu.get_barrier_semaphore()
    for other in (partner, xn, yn):
        pl.semaphore_signal(barrier, inc=1, device_id=dev(other), device_id_type=MESH)
    pl.semaphore_wait(barrier, 3)

    def chunk(i):
        rows = size(i)
        final = isinstance(i, int)
        prev = i - 1 if not final else jnp.int32(i - 1)
        later = True if final else i > 0
        x_copy(i).wait()
        if not final:
            when(i + 1 < n_main, lambda: x_copy(i + 1).start())
            when(i + 1 == n_main, lambda: x_copy(n_main).start())
        xs = lax.rem(jnp.int32(i), 2)

        def gu(j):
            g = i * n_gu + j

            def reduce():
                def span(at, start, f, each=2):
                    lo = start + each * jnp.maximum(j - at, 0)
                    hi = start + each * jnp.maximum(j - at + 1, 0)
                    loop(jnp.minimum(lo, n_u), jnp.minimum(hi, n_u), lambda u: f(prev, u))

                span(0, p1_left, p1)
                span(P2_AT, 0, p2)
                span(P3_AT, 0, p3, P3_EACH)

            when(later, reduce)
            slot = lax.rem(g, 2)
            for cp in gu_copies(g):
                cp.wait()
            r = jnp.dot(xbuf[xs, :rows], wgu[slot], preferred_element_type=F32)
            gate, up = r[:, :GT], r[:, GT:]
            at = pl.ds(pl.multiple_of(j * GT, GT), GT)
            hid[:rows, at] = (jax.nn.silu(gate) * up).astype(BF16)

            def fetch():
                for cp in gu_copies(g + 2):
                    cp.start()

            when(g + 2 < n_chunks * n_gu, fetch)

        loop(0, n_gu, gu)

        def product(g):
            return jnp.dot(hid[:rows, :], wdb[lax.rem(g, SLOTS)], preferred_element_type=F32)

        def next_wd(g):
            when(g + SLOTS < n_chunks * n_dn, lambda: wd_copy(g + SLOTS).start())

        def down(t, other, own):
            k, u = t, t - O_LEAD
            g_k, g_u = i * n_dn + o_index(k), i * n_dn + w_index(u)
            if other:
                def reuse():
                    o_send(prev, k).wait_send()
                    when(k == 0, lambda: pl.semaphore_wait(credit, 1))

                when(later, reuse)
                wd_copy(g_k).wait()
            if own:
                when(later, lambda: p4(prev, u))
                wd_copy(g_u).wait()
                o_send(i, u).wait_recv()
            if other:
                obuf[k, :rows] = product(g_k).astype(BF16)
            if own:
                total = (product(g_u) + orecv[u, :rows].astype(F32)).astype(BF16)
                for k2 in range(2):
                    sbuf[k2, u, :rows] = total[:, k2 * V : (k2 + 1) * V]
            if other:
                o_send(i, k).start()
                next_wd(g_k)
            if own:
                for k2 in range(2):
                    rs1(i, k2, u).start()
                next_wd(g_u)
                if final:
                    when(t >= END_P1, lambda: p1(i, t - END_P1))
                    when(t >= END_P2, lambda: p2(i, t - END_P2))
                else:
                    when(t >= P1_LAG, lambda: p1(i, t - P1_LAG))

        loop(0, O_LEAD, lambda t: down(t, True, False))
        loop(O_LEAD, n_u, lambda t: down(t, True, True))
        loop(n_u, n_u + O_LEAD, lambda t: down(t, False, True))
        if not final:
            pl.semaphore_signal(credit, inc=1, device_id=dev(partner), device_id_type=MESH)

    loop(0, n_main, chunk)
    chunk(n_main)

    def tail(s):
        when(jnp.logical_and(s >= p1_end, s < n_u), lambda: p1(n_main, s))
        when(jnp.logical_and(s >= p2_end + D2, s < n_u + D2), lambda: p2(n_main, s - D2))
        when(jnp.logical_and(s >= D3, s < n_u + D3), lambda: p3(n_main, s - D3))
        when(s >= D4, lambda: p4(n_main, s - D4))

    p1_end, p2_end = n_u + O_LEAD - END_P1, max(n_u + O_LEAD - END_P2, 0)
    loop(min(p1_end, p2_end + D2, D3), n_u + D4, tail)

    def drain(u):
        o_send(n_main, u).wait_send()

        def one(i):
            across(i, u).wait_send()
            across(i, u).wait_recv()

        loop(0, n_main, one)
        one(n_main)

    loop(0, n_u, drain)


def solution(mesh):
    def step(x, w_gate, w_up, w_down):
        rows, d = x.shape
        ff = w_gate.shape[1]
        n_main, n_gu, n_u = (rows - LAST) // MAIN, ff // GT, d // (2 * W)
        dma = pltpu.SemaphoreType.DMA
        pair = (2, n_u)
        any_space = pl.BlockSpec(memory_space=pl.ANY)
        return pl.pallas_call(
            functools.partial(kernel, n_main, n_gu, n_u),
            out_shape=jax.ShapeDtypeStruct((rows, d), BF16),
            in_specs=[any_space] * 4,
            out_specs=any_space,
            scratch_shapes=[
                pltpu.VMEM((2, MAIN, d), BF16),
                pltpu.VMEM((MAIN, ff), BF16),
                pltpu.VMEM((2, d, 2 * GT), BF16),
                pltpu.VMEM((SLOTS, ff, W), BF16),
                pltpu.VMEM((n_u, MAIN, W), BF16),
                pltpu.VMEM((n_u, MAIN, W), BF16),
                pltpu.VMEM((2, n_u, MAIN, V), BF16),
                pltpu.VMEM((2, n_u, MAIN // 2, V), BF16),
                pltpu.VMEM((2, n_u, MAIN // 4, V), BF16),
                dma((2,)), dma((2, 2)), dma((SLOTS,)),
                dma((n_u,)), dma((n_u,)),
                *[dma(pair) for _ in range(10)],
                dma(pair),
                dma((n_main + 1, n_u)), dma((n_main + 1, n_u)),
                pltpu.SemaphoreType.REGULAR,
            ],
            compiler_params=pltpu.CompilerParams(
                collective_id=0, has_side_effects=True, vmem_limit_bytes=62 * 1024 * 1024
            ),
            name="mlp_reduce",
        )(x, w_gate, w_up, w_down)

    return jax.shard_map(
        step,
        mesh=mesh,
        in_specs=(P("dp", None), P(None, "tp"), P(None, "tp"), P("tp", None)),
        out_specs=P("dp", None),
        check_vma=False,
    )
```

time: 639 us -> 327 us (0.51)
  waiting for transfers between devices: 344 us -> 0 us
  Pallas kernels: 0 us -> 307 us
  matrix products: 262 us -> 0 us
  between operations: 13.4 us -> 0.01 us
    psum x1 -> x0, waiting for transfers between devices: 344 us -> none  [step(): return lax.psum(term, 'tp')]
    pallas_call x0 -> x1, Pallas kernels: none -> 307 us  [step(): pl.pallas_call(functools.partial(kernel, n_main, n_gu, n_u), out_shape=ja...]
    dot_general x3 -> x0, matrix products: 262 us -> none  [the longest x1 91.4 us: step(): up = jnp.dot(x, w_up, preferred_element_type=jnp.float32)]
  transfers between devices with their start and end apart: 1 -> 0, of which waited for: 1 -> 0; matrix products, arithmetic and copies ran while one was open for 0% -> 0% of each run, Pallas kernels for 0% -> 0%
where the time goes in v3:
time: 327 us
  Pallas kernels  307 us (94%)
  local copies, waits for them, and re-layouts  20.2 us (6%)
    pallas_call x1, Pallas kernels, step(): pl.pallas_call(functools.partial(kernel, n_main, n_gu, n_u), out_shape=ja...  307 us
    unnamed x1, local copies, waits for them, and re-layouts  20.2 us

profile of v3, /device:TPU:0, one launch (start us, length us, event | category | flops | bytes accessed | tf_op | source)
XLA Modules:
  0.0 327.3 jit_solution(13179336621152353783)
XLA Ops:
  0.0 307.2 %mlp_reduce.1 = bf16[2048,7168]{1,0:T(8,128)(2,1)} custom-call(bf16[2048,7168]{1,0:T(8,128)(2,1)} %x_hbm.1, bf16[7168,2560]{1,0:T(8,128)(2,1)} %wg_hbm.1, bf16[7168,2560]{1,0:T(8,128)(2,1)} %wu_hbm.1, bf16[2560,7168]{1,0:T(8,128)(2,1)} %wd_hbm.1), custom_call_target="tpu_custom_call" | custom-call | tf_op jit(solution)/shard_map/mlp_reduce/pallas_call | solution.py:338
  307.2 20.2 %copy.6 = bf16[2048,7168]{1,0:T(8,128)(2,1)} copy(bf16[2048,7168]{1,0:T(8,128)(2,1)} %mlp_reduce.1) | data formatting | bytes 58720256

commit v4 on v3

--- a/solution.py
+++ b/solution.py
@@ -18,7 +18,7 @@
 D2, D3, D4 = 1, 3, 5
 O_LEAD = 2
 P1_LAG = 8
-P2_AT, P3_AT, P3_EACH = 3, 8, 4
+P2_AT, P3_AT, P3_EACH = 3, 9, 7
 MESH = pl.DeviceIdType.MESH
 
 
@@ -183,6 +183,7 @@
             rows = pl.ds(keep2(i, k), q)
             sbuf[k, u, rows, :] = (sbuf[k, u, rows, :].astype(F32) + r2[k, u, :q].astype(F32)).astype(BF16)
             ag1(i, k, u).start()
+        for k in range(2):
             ag2(i, k, u).start()
             local(i, k, u).start()
 
@@ -206,11 +207,8 @@
     p1_left = n_u + O_LEAD - P1_LAG
 
     x_copy(0).start()
-    for g in range(2):
-        for cp in gu_copies(g):
-            cp.start()
-    for g in range(SLOTS):
-        wd_copy(g).start()
+    for cp in gu_copies(0):
+        cp.start()
     barrier = pltpu.get_barrier_semaphore()
     for other in (partner, xn, yn):
         pl.semaphore_signal(barrier, inc=1, device_id=dev(other), device_id_type=MESH)
@@ -222,9 +220,6 @@
         prev = i - 1 if not final else jnp.int32(i - 1)
         later = True if final else i > 0
         x_copy(i).wait()
-        if not final:
-            when(i + 1 < n_main, lambda: x_copy(i + 1).start())
-            when(i + 1 == n_main, lambda: x_copy(n_main).start())
         xs = lax.rem(jnp.int32(i), 2)
 
         def gu(j):
@@ -244,6 +239,19 @@
             slot = lax.rem(g, 2)
             for cp in gu_copies(g):
                 cp.wait()
+            if not final:
+                def second():
+                    for cp in gu_copies(1):
+                        cp.start()
+
+                def downs():
+                    for n in range(SLOTS):
+                        wd_copy(n).start()
+
+                when(g == 0, second)
+                when(g == 3, downs)
+                when(jnp.logical_and(j == 5, i + 1 < n_main), lambda: x_copy(i + 1).start())
+                when(jnp.logical_and(j == 5, i + 1 == n_main), lambda: x_copy(n_main).start())
             r = jnp.dot(xbuf[xs, :rows], wgu[slot], preferred_element_type=F32)
             gate, up = r[:, :GT], r[:, GT:]
             at = pl.ds(pl.multiple_of(j * GT, GT), GT)

time: 327 us -> 325 us (level)
  no operation moved by 1% of the time
where the time goes in v4:
time: 325 us
  Pallas kernels  305 us (94%)
  local copies, waits for them, and re-layouts  20.2 us (6%)
    pallas_call x1, Pallas kernels, step(): pl.pallas_call(functools.partial(kernel, n_main, n_gu, n_u), out_shape=ja...  305 us
    unnamed x1, local copies, waits for them, and re-layouts  20.2 us

profile of v4, /device:TPU:0, one launch (start us, length us, event | category | flops | bytes accessed | tf_op | source)
XLA Modules:
  0.0 324.8 jit_solution(533936750448896083)
XLA Ops:
  0.0 304.7 %mlp_reduce.1 = bf16[2048,7168]{1,0:T(8,128)(2,1)} custom-call(bf16[2048,7168]{1,0:T(8,128)(2,1)} %x_hbm.1, bf16[7168,2560]{1,0:T(8,128)(2,1)} %wg_hbm.1, bf16[7168,2560]{1,0:T(8,128)(2,1)} %wu_hbm.1, bf16[2560,7168]{1,0:T(8,128)(2,1)} %wd_hbm.1), custom_call_target="tpu_custom_call" | custom-call | tf_op jit(solution)/shard_map/mlp_reduce/pallas_call | solution.py:346
  304.7 20.2 %copy.6 = bf16[2048,7168]{1,0:T(8,128)(2,1)} copy(bf16[2048,7168]{1,0:T(8,128)(2,1)} %mlp_reduce.1) | data formatting | bytes 58720256
